TPU v7x, 32 devices: a whole 2x2x4 slice. The times are simulated.
32 devices in a mesh: cuts: 8 (over z, x), mode: 4 (over y, core).
Axes of the slice: x: 2, y: 2, z: 4, core: 2. Of those that a mesh axis runs over, the one named last changes fastest.
Arguments:
- sliced_state: bfloat16 [8, 16, 4, 128, 2, 128], P(None, 'cuts', None, 'mode'), may hold values from -0.75 to 0.75
- gate_blocks: bfloat16 [32, 2, 128, 128], P('cuts'), may hold values from -0.375 to 0.375
- gate_slot: int32 [32], replicated, may hold values from 0 to 31, each once
- samples: int32 [8, 4096], replicated, may hold values from 0 to 65535
Outputs:
- amplitudes: float32 [32, 128, 2, 128], P('cuts', 'mode')
- sample_probs: float32 [8, 4096], replicated
- xeb_score: float32 [8], replicated
Inputs may be any that keep to these rules, and one draw needn't show every extreme that they name: `gate_slot`: a permutation: every gate block has its own row of gate_blocks. `samples`: flat index s * 128 * 128 + p * 128 + q.
All inputs are finite; a program needn't handle non-finite values.
Results may differ from a plain program's by a relative error of at most 0.022.
Values may be sent and summed in bfloat16 or wider, within the bound.
A program may use at most 64 MiB of HBM per device.

v0:
```python
import jax
import jax.numpy as jnp
from jax import lax
from jax.sharding import PartitionSpec as P


def from_root(array, axis, root):
    mine = lax.axis_index(axis) == root
    return lax.psum(jnp.where(mine, array, jnp.zeros_like(array)), axis)


def apply_gates(tensor, blocks):
    real_part = blocks[:, 0]
    imag_part = blocks[:, 1]
    stacked = jnp.concatenate(
        [
            jnp.concatenate([real_part, imag_part], axis=2),
            jnp.concatenate([-imag_part, real_part], axis=2),
        ],
        axis=1,
    )
    layout = tensor.shape
    flattened = tensor.reshape(layout[0], -1, 2 * layout[-1])
    product = jnp.einsum("crk,ckn->crn", flattened, stacked, preferred_element_type=jnp.float32)
    return product.astype(jnp.bfloat16).reshape(layout)


def select_rows(table, wanted):
    count = table.shape[0]
    onehot = (wanted[:, None] == jnp.arange(count, dtype=jnp.int32)[None, :]).astype(table.dtype)
    picked = jnp.dot(onehot, table.reshape(count, -1), preferred_element_type=jnp.float32)
    return picked.astype(table.dtype).reshape((wanted.shape[0],) + table.shape[1:])


def on_device(sliced_state, gate_blocks, gate_slot, samples):
    circuits = sliced_state.shape[0]
    spectator = sliced_state.shape[2]
    width = sliced_state.shape[5]
    held_count = gate_blocks.shape[0]
    layer_count = gate_slot.shape[0] // (2 * circuits)
    circuit_ids = jnp.arange(circuits, dtype=jnp.int32)
    tensor = lax.all_to_all(sliced_state, "mode", split_axis=0, concat_axis=3, tiled=True)
    local_count = tensor.shape[0]
    local_ids = lax.axis_index("mode") * local_count + jnp.arange(local_count, dtype=jnp.int32)

    def fetch_one(position):
        held_block = select_rows(gate_blocks, jnp.reshape(position % held_count, (1,)))[0]
        return from_root(held_block, "cuts", position // held_count)

    def fetch_gates(layer_index, gate_kind):
        fetched = []
        for circuit in range(local_count):
            fetched.append(
                fetch_one(
                    gate_slot[(local_ids[circuit] * layer_count + layer_index) * 2 + gate_kind]
                )
            )
        return jnp.stack(fetched, axis=0)

    for layer_index in range(layer_count):
        tensor = apply_gates(tensor, fetch_gates(layer_index, 0))
        tensor = jnp.swapaxes(tensor, 3, 5)
        tensor = apply_gates(tensor, fetch_gates(layer_index, 1))
        tensor = jnp.swapaxes(tensor, 3, 5)
    summed = jnp.sum(tensor.astype(jnp.float32), axis=1)
    summed = lax.all_to_all(
        summed.astype(jnp.bfloat16), "mode", split_axis=2, concat_axis=0, tiled=True
    ).astype(summed.dtype)
    local_rows = summed.shape[2]
    summed = summed.reshape(circuits * spectator, local_rows, 2, width)
    amplitudes = lax.psum_scatter(
        summed.astype(jnp.bfloat16), "cuts", scatter_dimension=0, tiled=True
    ).astype(jnp.float32)
    row_count = amplitudes.shape[0]
    first_row = lax.axis_index("cuts") * row_count
    first_col = lax.axis_index("mode") * local_rows
    magnitude = amplitudes[:, :, 0, :] ** 2 + amplitudes[:, :, 1, :] ** 2
    row_sums = jnp.sum(magnitude, axis=(1, 2))
    owner_circuit = (first_row + jnp.arange(row_count, dtype=jnp.int32)) // spectator
    norm_part = jnp.sum(
        jnp.where(owner_circuit[None, :] == circuit_ids[:, None], row_sums[None, :], 0.0), axis=1
    )
    plane_size = width * width
    spec_index = samples // plane_size
    row_index = samples // width % width
    col_index = samples % width
    local_row = circuit_ids[:, None] * spectator + spec_index - first_row
    local_col = row_index - first_col
    is_owned = (
        (local_row >= 0) & (local_row < row_count) & (local_col >= 0) & (local_col < local_rows)
    )
    cell_index = jnp.where(is_owned, local_row * local_rows + local_col, -1)
    cell_count = row_count * local_rows
    cell_onehot = (
        cell_index[:, :, None] == jnp.arange(cell_count, dtype=jnp.int32)[None, None, :]
    ).astype(jnp.float32)
    picked_rows = jnp.einsum(
        "csr,rw->csw",
        cell_onehot,
        magnitude.reshape(cell_count, width),
        precision=lax.Precision.HIGHEST,
    )
    col_match = col_index[:, :, None] == jnp.arange(width, dtype=jnp.int32)[None, None, :]
    sample_mass = jnp.sum(jnp.where(col_match, picked_rows, 0.0), axis=2)
    dimension_scale = float(spectator * plane_size)
    norm_total = lax.psum(norm_part, ("cuts", "mode"))
    sample_probs = lax.psum(sample_mass * dimension_scale / norm_total[:, None], ("cuts", "mode"))
    xeb_score = jnp.mean(sample_probs, axis=1)
    return (amplitudes, sample_probs, xeb_score)


def solution(mesh):
    in_specs = (P(None, "cuts", None, "mode", None, None), P("cuts", None, None, None), P(), P())
    out_specs = (P("cuts", "mode", None, None), P(), P())
    return jax.shard_map(
        on_device, mesh=mesh, in_specs=in_specs, out_specs=out_specs, check_vma=False
    )
```

profile of v0, /device:TPU:0, one launch (start us, length us, event | category | flops | bytes accessed | tf_op | source)
XLA Modules:
  0.0 402.5 jit_solution(14701239896464762398)
XLA Ops:
  7.2 0.6 fusion.74
  10.4 1.6 fusion.73
  32.4 1.2 copy.56
  33.9 0.7 copy.39
  35.0 0.7 copy.40
  37.7 0.6 convert_select_fusion.5
  38.3 0.6 convert_select_fusion.4
  39.0 0.6 convert_select_fusion.3
  39.6 0.6 convert_select_fusion.2
  40.2 0.6 convert_select_fusion.1
  40.8 0.6 convert_select_fusion
  41.5 4.3 %all-to-all-start = ((bf16[8,2,4,32,2,128]{5,4,3,2,1,0:T(2,128)(2,1)}), bf16[8,2,4,32,2,128]{5,4,3,2,1,0:T(2,128)(2,1)S(1)}, u32[]{:S(2)}, u32[]{:S(2)}) async-start(bf16[8,2,4,32,2,128]{5,4,3,2,1,0:T(2,128)(2,1)} %param.4), calls=%async_computation | async-start | bytes 2097152 | tf_op jit(solution)/shard_map/all_to_all | solution.py:42
  45.8 72.8 %all-reduce.6.cloned.1.call-done = (bf16[1,2,128,128]{2,3,0,1:T(8,128)(2,1)}, bf16[1,2,128,128]{2,3,0,1:T(8,128)(2,1)}, bf16[1,2,128,128]{3,2,0,1:T(8,128)(2,1)}...) async-done(((bf16[1,2,128,128]{2,3,0,1:T(8,128)(2,1)}, ...) | async-done | bytes 524304 | tf_op jit(solution)/shard_map/psum | solution.py:9
  118.6 0.9 constant_dynamic-update-slice_fusion.1
  119.5 0.9 constant_dynamic-update-slice_fusion
  120.4 0.8 constant_dynamic-update-slice_fusion.3
  121.2 0.8 constant_dynamic-update-slice_fusion.5
  122.1 0.9 constant_dynamic-update-slice_fusion.2
  123.1 1.2 copy.55
  124.4 0.7 reshape.305
  125.1 0.5 fusion.2
  125.5 0.8 reshape.306
  126.3 1.1 copy.42
  127.4 0.7 reshape.307
  128.1 0.4 convolution_convert_fusion.2
  128.6 0.3 reshape.308
  128.9 1.2 copy.43
  130.1 0.7 reshape.309
  130.8 0.4 convolution_convert_fusion.1
  131.2 0.3 reshape.310
  131.5 1.2 copy.44
  132.8 0.7 reshape.311
  133.5 0.4 convolution_convert_fusion
  133.9 0.3 reshape.312
  134.2 2.4 reduce_sum.50
  136.7 0.7 copy.45
  137.4 11.4 %all_to_all.33 = bf16[2,4,128,2,128]{4,3,1,0,2:T(2,128)(2,1)S(1)} all-to-all(bf16[2,4,128,2,128]{4,3,1,0,2:T(2,128)(2,1)S(1)} %copy.45), channel_id=1, replica_groups=mesh['cuts'=8,'mode'=4] {'mode'}, dimensions={2} | all-to-all | bytes 1048576 | tf_op jit(solution)/shard_map/all_to_all | solution.py:66
  148.9 0.8 copy.47
  149.9 61.7 %reduce-scatter.2.cloned.1.call-done = bf16[4,32,2,128]{3,1,2,0:T(8,128)(2,1)} async-done(((bf16[32,32,2,128]{3,1,2,0:T(8,128)(2,1)}), bf16[4,32,2,128]{3,1,2,0:T(8,128)(2,1)}) %reduce-scatter.2.cloned.1.call-update) | async-done | bytes 65552 | tf_op jit(solution)/shard_map/reduce_scatter | solution.py:71
  211.5 0.8 convert_element_type.77
  212.9 40.1 %psum.78 = f32[8]{0:T(128)S(1)} all-reduce(f32[8]{0:T(128)S(1)} %select_reduce_fusion.1), channel_id=1, replica_groups=mesh['cuts'=8,'mode'=4] {'cuts','mode'}, use_global_device_ids=true, to_apply=%region_13.14 | all-reduce | flops 8 | bytes 64 | tf_op jit(solution)/shard_map/psum | solution.py:106
  252.9 15.4 %select_reduce_fusion = f32[8,4096]{1,0:T(8,128)S(1)} fusion(s32[8,4096]{1,0:T(8,128)S(1)} %get-tuple-element.23, f32[128,128,1]{1,0,2:T(8,128)S(1)} %bitcast.154, s32[8,4096]{1,0:T(8,128)S(1)} %get-tuple-element.22), kind=kOutput, calls=%fused_computation | convolution fusion | flops 6459195392 | bytes 458752 | tf_op jit(solution)/shard_map/csr,rw->csw/dot_general | solution.py:97
  268.4 0.7 multiply_divide_fusion
  269.2 0.7 copy.49
  269.9 123.0 %all-reduce.4.cloned.1.call-done = f32[8,4096]{1,0:T(8,128)} async-done(((f32[8,4096]{1,0:T(8,128)}), f32[8,4096]{1,0:T(8,128)}) %all-reduce.4.cloned.1.call-update) | async-done | bytes 131088 | tf_op jit(solution)/shard_map/psum | solution.py:107
  392.8 1.1 reduce_sum.55
  393.9 0.5 broadcast_multiply_fusion
  394.4 1.6 copy.70
  (42 shorter events, 3.2 us)
Async XLA Ops:
  7.2 111.4 %all-reduce.6.cloned.1.call-start = ((), (), s32[]{:S(2)}) async-start(), calls=%async_computation.5 | async-start | bytes 1048576 | tf_op jit(solution)/shard_map/psum | solution.py:9
  41.5 81.6 %all-to-all-start = ((bf16[8,2,4,32,2,128]{5,4,3,2,1,0:T(2,128)(2,1)}), bf16[8,2,4,32,2,128]{5,4,3,2,1,0:T(2,128)(2,1)S(1)}, u32[]{:S(2)}, u32[]{:S(2)}) async-start(bf16[8,2,4,32,2,128]{5,4,3,2,1,0:T(2,128)(2,1)} %param.4), calls=%async_computation | async-start | bytes 2097152 | tf_op jit(solution)/shard_map/all_to_all | solution.py:42
  45.8 165.8 %reduce-scatter.2.cloned.1.call-start = ((), (), s32[]{:S(2)}) async-start(), calls=%async_computation.3 | async-start | bytes 589824 | tf_op jit(solution)/shard_map/reduce_scatter | solution.py:71
  118.6 4.4 %copy-start.3 = (bf16[1,2,128,128]{3,2,0,1:T(8,128)(2,1)S(1)}, bf16[1,2,128,128]{3,2,0,1:T(8,128)(2,1)}, u32[]{:S(2)}) copy-start(bf16[1,2,128,128]{3,2,0,1:T(8,128)(2,1)} %get-tuple-element.18) | copy-start | bytes 196612
  118.6 4.4 %copy-start.2 = (bf16[1,2,128,128]{3,2,0,1:T(8,128)(2,1)S(1)}, bf16[1,2,128,128]{3,2,0,1:T(8,128)(2,1)}, u32[]{:S(2)}) copy-start(bf16[1,2,128,128]{3,2,0,1:T(8,128)(2,1)} %get-tuple-element.19) | copy-start | bytes 196612
  148.9 63.7 %copy-start.1 = (s32[8,4096]{1,0:T(8,128)S(1)}, s32[8,4096]{1,0:T(8,128)}, u32[]{:S(2)}) copy-start(s32[8,4096]{1,0:T(8,128)} %param.7) | copy-start | bytes 393220
  149.8 243.0 %all-reduce.4.cloned.1.call-start = ((), (), s32[]{:S(2)}) async-start(), calls=%async_computation.4 | async-start | bytes 262144 | tf_op jit(solution)/shard_map/psum | solution.py:107
  252.9 16.2 %copy-start = (bf16[4,32,2,128]{3,1,2,0:T(8,128)(2,1)S(1)}, bf16[4,32,2,128]{3,1,2,0:T(8,128)(2,1)}, u32[]{:S(2)}) copy-start(bf16[4,32,2,128]{3,1,2,0:T(8,128)(2,1)} %reduce-scatter.2.cloned.1.call-done) | copy-start | bytes 196612
Sparse Core Ops, SparseCore 0:
  41.6 76.9 all-reduce.5
  149.9 61.5 reduce-scatter.1
  269.3 123.5 all-reduce.3
where the time goes:
time: 403 us; the launch traced here: 402 us
  waiting for transfers between devices  257 us (64%)
  blocking collectives  51.4 us (13%)
  between operations  37.4 us (9%)
  local copies, waits for them, and re-layouts  22.5 us (6%)
  matrix products  19.5 us (5%)
  other arithmetic  9.91 us (2%)
  starting transfers between devices  4.36 us (1%)
    psum x1, waiting for transfers between devices, on_device(): lax.psum(sample_mass * dimension_scale / norm_total[:, None], ('cuts', 'm...  123 us
    psum x1, waiting for transfers between devices, from_root(): return lax.psum(jnp.where(mine, array, jnp.zeros_like(array)), axis)  72.8 us
    reduce_scatter x1, waiting for transfers between devices, on_device(): lax.psum_scatter(summed.astype(jnp.bfloat16), 'cuts', scatter_dimension=0...  61.7 us
    psum x1, blocking collectives, on_device(): norm_total = lax.psum(norm_part, ('cuts', 'mode'))  40.1 us
    dot_general x1, matrix products, on_device(): jnp.einsum('csr,rw->csw', cell_onehot, magnitude.reshape(cell_count, widt...  15.4 us
    all_to_all x1, blocking collectives, on_device(): lax.all_to_all(summed.astype(jnp.bfloat16), 'mode', split_axis=2, concat_...  11.4 us
  transfers between devices with their start and end apart: 4, of which 3 were waited for; matrix products, arithmetic and copies ran while one was open for 1% of the time, Pallas kernels for 0%

commit v1 on v0

--- a/solution.py
+++ b/solution.py
@@ -104,7 +104,9 @@
     sample_mass = jnp.sum(jnp.where(col_match, picked_rows, 0.0), axis=2)
     dimension_scale = float(spectator * plane_size)
     norm_total = lax.psum(norm_part, ("cuts", "mode"))
-    sample_probs = lax.psum(sample_mass * dimension_scale / norm_total[:, None], ("cuts", "mode"))
+    part = sample_mass * dimension_scale / norm_total[:, None]
+    parts = lax.all_gather(part, ("cuts", "mode"))
+    sample_probs = jnp.sum(parts, axis=0)
     xeb_score = jnp.mean(sample_probs, axis=1)
     return (amplitudes, sample_probs, xeb_score)
 

time: 403 us -> 344 us (0.85)
  waiting for transfers between devices: 257 us -> 195 us
    psum x1 -> x0, waiting for transfers between devices: 123 us -> none  [on_device(): lax.psum(sample_mass * dimension_scale / norm_total[:, None], ('cuts', 'm...]
    all_gather x0 -> x1, waiting for transfers between devices: none -> 60.1 us  [on_device(): parts = lax.all_gather(part, ('cuts', 'mode'))]
  transfers between devices with their start and end apart: 4 -> 4, of which waited for: 3 -> 3; matrix products, arithmetic and copies ran while one was open for 1% -> 2% of each run, Pallas kernels for 0% -> 0%
where the time goes in v1:
time: 344 us; the launch traced here: 343 us
  waiting for transfers between devices  195 us (57%)
  blocking collectives  51.7 us (15%)
  between operations  37.3 us (11%)
  local copies, waits for them, and re-layouts  22.6 us (7%)
  matrix products  19.5 us (6%)
  other arithmetic  12.8 us (4%)
  starting transfers between devices  4.36 us (1%)
    psum x1, waiting for transfers between devices, from_root(): return lax.psum(jnp.where(mine, array, jnp.zeros_like(array)), axis)  72.8 us
    reduce_scatter x1, waiting for transfers between devices, on_device(): lax.psum_scatter(summed.astype(jnp.bfloat16), 'cuts', scatter_dimension=0...  61.6 us
    all_gather x1, waiting for transfers between devices, on_device(): parts = lax.all_gather(part, ('cuts', 'mode'))  60.1 us
    psum x1, blocking collectives, on_device(): norm_total = lax.psum(norm_part, ('cuts', 'mode'))  40.3 us
    dot_general x1, matrix products, on_device(): jnp.einsum('csr,rw->csw', cell_onehot, magnitude.reshape(cell_count, widt...  15.4 us
    all_to_all x1, blocking collectives, on_device(): lax.all_to_all(summed.astype(jnp.bfloat16), 'mode', split_axis=2, concat_...  11.4 us
  transfers between devices with their start and end apart: 4, of which 3 were waited for; matrix products, arithmetic and copies ran while one was open for 2% of the time, Pallas kernels for 0%

profile of v1, /device:TPU:0, one launch (start us, length us, event | category | flops | bytes accessed | tf_op | source)
XLA Modules:
  0.0 342.7 jit_solution(13683426155146345401)
XLA Ops:
  7.2 0.6 fusion.75
  10.4 1.6 fusion.74
  32.4 1.2 copy.56
  35.9 0.7 copy.40
  36.9 0.7 copy.39
  37.7 0.6 convert_select_fusion
  38.3 0.6 convert_select_fusion.1
  38.9 0.6 convert_select_fusion.2
  39.6 0.6 convert_select_fusion.3
  40.2 0.6 convert_select_fusion.4
  40.8 0.6 convert_select_fusion.5
  41.5 4.3 %all-to-all-start = ((bf16[8,2,4,32,2,128]{5,4,3,2,1,0:T(2,128)(2,1)}), bf16[8,2,4,32,2,128]{5,4,3,2,1,0:T(2,128)(2,1)S(1)}, u32[]{:S(2)}, u32[]{:S(2)}) async-start(bf16[8,2,4,32,2,128]{5,4,3,2,1,0:T(2,128)(2,1)} %param.4), calls=%async_computation | async-start | bytes 2097152 | tf_op jit(solution)/shard_map/all_to_all | solution.py:42
  45.7 72.8 %all-reduce.3.cloned.1.call-done = (bf16[1,2,128,128]{2,3,0,1:T(8,128)(2,1)}, bf16[1,2,128,128]{2,3,0,1:T(8,128)(2,1)}, bf16[1,2,128,128]{3,2,0,1:T(8,128)(2,1)}...) async-done(((bf16[1,2,128,128]{2,3,0,1:T(8,128)(2,1)}, ...) | async-done | bytes 524304 | tf_op jit(solution)/shard_map/psum | solution.py:9
  118.6 0.8 constant_dynamic-update-slice_fusion.3
  119.4 0.8 constant_dynamic-update-slice_fusion.5
  120.3 0.9 constant_dynamic-update-slice_fusion.2
  121.2 0.8 constant_dynamic-update-slice_fusion.1
  122.0 0.9 constant_dynamic-update-slice_fusion
  122.9 0.8 constant_dynamic-update-slice_fusion.7
  123.8 0.9 constant_dynamic-update-slice_fusion.6
  124.7 1.2 copy.55
  125.9 0.7 reshape.334
  126.7 0.5 fusion.2
  127.1 0.8 reshape.335
  127.9 1.1 copy.42
  129.0 0.7 reshape.336
  129.7 0.4 convolution_convert_fusion.2
  130.1 0.3 reshape.337
  130.4 1.2 copy.43
  131.7 0.7 reshape.338
  132.4 0.4 convolution_convert_fusion.1
  133.1 1.2 copy.44
  134.4 0.7 reshape.340
  135.1 0.4 convolution_convert_fusion
  135.5 0.3 reshape.341
  135.8 2.4 reduce_sum.59
  138.3 0.7 copy.45
  139.0 11.4 %all_to_all.33 = bf16[2,4,128,2,128]{4,3,1,0,2:T(2,128)(2,1)S(1)} all-to-all(bf16[2,4,128,2,128]{4,3,1,0,2:T(2,128)(2,1)S(1)} %copy.45), channel_id=1, replica_groups=mesh['cuts'=8,'mode'=4] {'mode'}, dimensions={2} | all-to-all | bytes 1048576 | tf_op jit(solution)/shard_map/all_to_all | solution.py:66
  150.5 0.8 copy.47
  151.5 61.6 %reduce-scatter.2.cloned.1.call-done = bf16[4,32,2,128]{3,1,2,0:T(8,128)(2,1)} async-done(((bf16[32,32,2,128]{3,1,2,0:T(8,128)(2,1)}), bf16[4,32,2,128]{3,1,2,0:T(8,128)(2,1)}) %reduce-scatter.2.cloned.1.call-update) | async-done | bytes 65552 | tf_op jit(solution)/shard_map/reduce_scatter | solution.py:71
  213.1 0.8 convert_element_type.77
  214.4 40.3 %psum.71 = f32[8]{0:T(128)S(1)} all-reduce(f32[8]{0:T(128)S(1)} %select_reduce_fusion.1), channel_id=1, replica_groups=mesh['cuts'=8,'mode'=4] {'cuts','mode'}, use_global_device_ids=true, to_apply=%region_13.14 | all-reduce | flops 8 | bytes 64 | tf_op jit(solution)/shard_map/psum | solution.py:106
  254.7 15.4 %select_reduce_fusion = f32[8,4096]{1,0:T(8,128)S(1)} fusion(s32[8,4096]{1,0:T(8,128)S(1)} %get-tuple-element.25, f32[128,128,1]{1,0,2:T(8,128)S(1)} %bitcast.156, s32[8,4096]{1,0:T(8,128)S(1)} %get-tuple-element.24), kind=kOutput, calls=%fused_computation | convolution fusion | flops 6459195392 | bytes 458752 | tf_op jit(solution)/shard_map/csr,rw->csw/dot_general | solution.py:97
  270.2 0.7 bitcast_divide_fusion
  271.0 0.7 copy.49
  271.7 60.1 %all-gather.2.cloned.1.call-done = f32[32,8,4096]{2,1,0:T(8,128)} async-done(((f32[1,8,4096]{2,1,0:T(8,128)}), f32[32,8,4096]{2,1,0:T(8,128)}) %all-gather.2.cloned.1.call-update) | async-done | bytes 4194320 | tf_op jit(solution)/shard_map/all_gather | solution.py:108
  331.7 4.0 %fusion.71 = (f32[8]{0:T(128)S(1)}, f32[8,4096]{1,0:T(8,128)}) fusion(f32[32,8,4096]{2,1,0:T(8,128)} %all-gather.2.cloned.1.call-done), kind=kLoop, calls=%fused_computation.137 | loop fusion | flops 2064376 | bytes 4325408 | tf_op jit(solution)/shard_map/reduce_sum | solution.py:110
  335.7 0.5 broadcast_multiply_fusion
  (37 shorter events, 3.5 us)
Async XLA Ops:
  7.2 111.4 %all-reduce.3.cloned.1.call-start = ((), (), s32[]{:S(2)}) async-start(), calls=%async_computation.5 | async-start | bytes 1048576 | tf_op jit(solution)/shard_map/psum | solution.py:9
  41.5 83.2 %all-to-all-start = ((bf16[8,2,4,32,2,128]{5,4,3,2,1,0:T(2,128)(2,1)}), bf16[8,2,4,32,2,128]{5,4,3,2,1,0:T(2,128)(2,1)S(1)}, u32[]{:S(2)}, u32[]{:S(2)}) async-start(bf16[8,2,4,32,2,128]{5,4,3,2,1,0:T(2,128)(2,1)} %param.4), calls=%async_computation | async-start | bytes 2097152 | tf_op jit(solution)/shard_map/all_to_all | solution.py:42
  45.7 167.3 %reduce-scatter.2.cloned.1.call-start = ((), (), s32[]{:S(2)}) async-start(), calls=%async_computation.3 | async-start | bytes 589824 | tf_op jit(solution)/shard_map/reduce_scatter | solution.py:71
  135.5 78.6 %copy-start.1 = (s32[8,4096]{1,0:T(8,128)S(1)}, s32[8,4096]{1,0:T(8,128)}, u32[]{:S(2)}) copy-start(s32[8,4096]{1,0:T(8,128)} %param.7) | copy-start | bytes 393220
  151.4 180.3 %all-gather.2.cloned.1.call-start = ((), (), s32[]{:S(2)}) async-start(), calls=%async_computation.4 | async-start | bytes 4325376 | tf_op jit(solution)/shard_map/all_gather | solution.py:108
  254.7 16.2 %copy-start = (bf16[4,32,2,128]{3,1,2,0:T(8,128)(2,1)S(1)}, bf16[4,32,2,128]{3,1,2,0:T(8,128)(2,1)}, u32[]{:S(2)}) copy-start(bf16[4,32,2,128]{3,1,2,0:T(8,128)(2,1)} %reduce-scatter.2.cloned.1.call-done) | copy-start | bytes 196612
Sparse Core Ops, SparseCore 0:
  41.6 76.9 all-reduce.2
  151.5 61.5 reduce-scatter.1
  271.1 60.6 all-gather.1
